TPU v7x, 512 devices: a whole 4x4x16 slice. The times are simulated.
512 devices in a mesh: segment: 16 (over z_hi, y, core), dp: 32 (over x, z_lo).
Axes of the slice: x: 4, y: 4, z: 16 (z_hi: 2, z_lo: 8; z = z_hi * 8 + z_lo), core: 2. Of those that a mesh axis runs over, the one named last changes fastest.
Arguments:
- token_ids: int32 [4096], P('dp'), may hold values from 0 to 152063, as said below
- table: bfloat16 [19008, 28672], P('segment', 'dp'), may hold values from -6 to 6
- out_grad: bfloat16 [4096, 3584], P('dp', 'segment'), may hold values from -6 to 6
Outputs:
- embedded: bfloat16 [4096, 3584], P('dp')
- table_grad: bfloat16 [19008, 28672], P('segment', 'dp')
Inputs may be any that keep to these rules, and one draw needn't show every extreme that they name: `token_ids`: in the 128 tokens of each data group, at most 16 ids lie in one segment's slice of 9504 rows with one residue modulo 8; in every data group some segment and residue has exactly 16.
All inputs are finite; a program needn't handle non-finite values.
Results may differ from a plain program's by a relative error of at most 0.001.
Values may be sent and summed in bfloat16 or wider, within the bound.
No kernel may reach another device: no remote copies, remote signals or barrier semaphores. Data moves between devices by JAX's collectives and lax.ppermute only.
A program may use at most 64 MiB of HBM per device.

v0:
```python
import itertools
import jax
import jax.numpy as jnp
from jax import lax
from jax.sharding import Mesh, PartitionSpec as P

D = 3584
PACK = 8
SLOTS = 16
NAMES = ("z_hi", "y", "core", "x", "z_lo")
SIZES = (2, 4, 2, 4, 8)
PLANE = ("y", "core", "x")
GROUPS = ("x", "z_lo")
QUARTERS = 4
WIDTH = D // QUARTERS
BF16 = jnp.bfloat16


def move(values, to):

    def flat(place):
        number = 0
        for size, at in zip(SIZES, place):
            number = number * size + at
        return number

    pairs = [
        (flat(place), flat(to(*place)))
        for place in itertools.product(*(range(size) for size in SIZES))
    ]
    return lax.ppermute(values, NAMES, pairs)


def lookup_code(z_hi, z_lo):
    return z_lo


def grad_code(z_hi, z_lo):
    return z_hi * 4 + z_lo // 4 * 2 + z_lo % 2


def grad_target(z_hi, y, core, x, z_lo):
    code = core * 4 + y ^ z_lo
    return (code // 4, y, core, x, code // 2 % 2 * 4 + 2 * z_hi + code % 2)


def groups_of_plane(code):
    at = jnp.arange(32, dtype=jnp.int32)
    y, core, x = (at // 8, at // 4 % 2, at % 4)
    return x * 8 + (core * 4 + y ^ code)


def pick_matrix(ids, section, z_hi, parity):
    segment = ids // section
    residue = ids % section % PACK
    bucket = segment * PACK + residue
    count = ids.shape[0]
    order = jnp.arange(count, dtype=jnp.int32)
    earlier = (bucket[:, None] == bucket[None, :]) & (order[None, :] < order[:, None])
    rank = jnp.sum(earlier.astype(jnp.int32), axis=1)
    here = (segment // 8 == z_hi) & (residue % 2 == parity)
    slot = jnp.where(here, (segment % 8 * 4 + residue // 2) * SLOTS + rank, -1)
    return (slot[:, None] == jnp.arange(32 * SLOTS, dtype=jnp.int32)[None, :]).astype(BF16)


def body(token_ids, table, out_grad):
    lines, width = table.shape
    section = lines * PACK
    tokens = token_ids.shape[0]
    z_hi, y, core, x, z_lo = (lax.axis_index(name) for name in NAMES)
    segment = (z_hi * 4 + y) * 2 + core
    residue = x * 2 + z_lo // 4
    parity = z_lo // 4
    place = core * 4 + y
    every_id = lax.all_to_all(
        jnp.broadcast_to(token_ids[None], (32, tokens)), GROUPS, 0, 0, tiled=True
    )
    code_f = lookup_code(z_hi, z_lo)
    code_b = grad_code(z_hi, z_lo)
    orders = jnp.concatenate([groups_of_plane(code_f), groups_of_plane(code_b)])
    ids = jnp.take(every_id, orders, axis=0)
    local = ids - segment * section
    owned = (local >= 0) & (local < section) & (local % PACK == residue)
    line = local // PACK
    steps = jnp.arange(tokens, dtype=jnp.int32)
    before = (steps[:, None] < steps[None, :]).astype(BF16)
    rank = jnp.dot(owned.astype(BF16), before, preferred_element_type=jnp.float32).astype(jnp.int32)
    slots = jnp.arange(SLOTS, dtype=jnp.int32)
    hit = owned[:, None, :] & (rank[:, None, :] == slots[None, :, None])
    row_of = jnp.sum(jnp.where(hit, line[:, None, :] + 1, 0), axis=2) - 1
    fetched = jnp.take(table, jnp.maximum(row_of[:32], 0).reshape(-1), axis=0)
    arrived = lax.all_to_all(fetched.reshape(32, SLOTS, width), PLANE, 0, 0, tiled=True)
    ids_f = lax.dynamic_index_in_dim(every_id, x * 8 + (place ^ code_f), 0, keepdims=False)
    pick_f = pick_matrix(ids_f, section, z_hi, parity)
    picked = jnp.dot(
        pick_f, arrived.reshape(32 * SLOTS, width), preferred_element_type=jnp.float32
    ).astype(BF16)

    def near(a, b, c, d, e):
        return (a, b, c, d, e ^ c * 4 + b)

    def far(a, b, c, d, e):
        return (1 - a, b, c, d, e ^ c * 4 + b)

    both = move(picked, near) + move(picked, far)
    quarter = both + lax.ppermute(both, "core", [(0, 1), (1, 0)])
    whole = lax.all_gather(quarter, "y")
    embedded = jnp.concatenate(
        [
            lax.dynamic_index_in_dim(whole, z_lo % 4 ^ part, 0, keepdims=False)
            for part in range(QUARTERS)
        ],
        axis=1,
    )
    halves = lax.all_gather(out_grad, ("y", "core"), axis=1, tiled=True)
    which = (place ^ z_lo) % 2
    piece = lax.dynamic_slice(halves, (0, which * width), (tokens, width))
    piece = move(piece, grad_target)
    ids_b = lax.dynamic_index_in_dim(every_id, x * 8 + (place ^ code_b), 0, keepdims=False)
    pick_b = pick_matrix(ids_b, section, z_hi, parity)
    packed = lax.dot_general(
        pick_b, piece, (((0,), (0,)), ((), ())), preferred_element_type=jnp.float32
    ).astype(BF16)
    returned = lax.all_to_all(packed.reshape(32, SLOTS, width), PLANE, 0, 0, tiled=True)
    target = row_of[32:].reshape(-1)
    spread = (jnp.arange(lines, dtype=jnp.int32)[:, None] == target[None, :]).astype(BF16)
    table_grad = jnp.dot(
        spread, returned.reshape(32 * SLOTS, width), preferred_element_type=jnp.float32
    ).astype(BF16)
    return (embedded, table_grad)


def solution(mesh):
    fine = Mesh(mesh.devices.reshape(SIZES), NAMES)
    segment, groups = (("z_hi", "y", "core"), ("x", "z_lo"))
    return jax.shard_map(
        body,
        mesh=fine,
        in_specs=(P(groups), P(segment, groups), P(groups, segment)),
        out_specs=(P(groups, None), P(segment, groups)),
        check_vma=False,
    )
```

profile of v0, /device:TPU:2, one launch (start us, length us, event | category | flops | bytes accessed | tf_op | source)
XLA Modules:
  0.0 144.1 jit_solution(15806224102012464601)
XLA Ops:
  0.6 1.4 broadcast_in_dim.37
  2.1 15.7 %all-to-all-start = ((s32[32,1,128]{2,1,0:T(1,128)}), s32[32,1,128]{2,1,0:T(1,128)S(1)}, u32[]{:S(2)}, u32[]{:S(2)}) async-start(s32[32,1,128]{2,1,0:T(1,128)} %broadcast_in_dim.37), calls=%async_computation | async-start | bytes 32768 | tf_op jit(solution)/shard_map/all_to_all | solution.py:75
  17.8 0.1 fusion.25
  17.9 0.1 compare_and_fusion
  18.0 11.0 %all-to-all-done = s32[32,1,128]{2,1,0:T(1,128)S(1)} async-done(((s32[32,1,128]{2,1,0:T(1,128)}), s32[32,1,128]{2,1,0:T(1,128)S(1)}, u32[]{:S(2)}, u32[]{:S(2)}) %all-to-all-start) | async-done | bytes 16416 | tf_op jit(solution)/shard_map/all_to_all | solution.py:75
  29.0 0.6 gather_fusion
  29.6 0.1 fusion.9
  29.7 0.1 fusion.11
  29.8 0.1 convolution_convert_fusion.3
  30.0 1.2 select_reduce_fusion
  31.2 0.1 reshape.480
  31.3 2.1 %gather_fusion.1 = bf16[512,896]{1,0:T(8,128)(2,1)S(1)} fusion(bf16[1188,896]{1,0:T(8,128)(2,1)S(1)} %copy-done, s32[1024]{0:T(1024)S(1)} %pad_clamp_fusion), kind=kCustom, calls=%fused_computation.1 | custom fusion | bytes 1837056 | tf_op jit(solution)/shard_map/jit(_take)/gather | solution.py:91
  33.3 1.1 broadcast_select_fusion
  34.4 6.7 %all-to-all-start.1 = ((bf16[32,16,896]{2,1,0:T(8,128)(2,1)}), bf16[32,16,896]{2,1,0:T(8,128)(2,1)S(1)}, u32[]{:S(2)}, u32[]{:S(2)}) async-start(bf16[32,16,896]{2,1,0:T(8,128)(2,1)} %broadcast_select_fusion), calls=%async_computation.1 | async-start | bytes 1835008 | tf_op jit(solution)/shard_map/all_to_all | solution.py:92
  41.2 21.6 %all_gather.11 = bf16[128,1792]{0,1:T(8,128)(2,1)S(1)} all-gather(bf16[128,224]{0,1:T(8,128)(2,1)} %param.5), channel_id=1, replica_groups=mesh['z_hi'=2,'y'=4,'core'=2,'x'=4,'z_lo'=8] {'y','core'}, dimensions={1}, use_global_device_ids=true | all-gather | bytes 516096 | tf_op jit(solution)/shard_map/all_gather | solution.py:115
  62.8 0.7 constant_dynamic-slice_fusion
  63.5 1.6 %collective-permute-start.3 = (bf16[128,896]{0,1:T(8,128)(2,1)}, bf16[128,896]{0,1:T(8,128)(2,1)S(1)}, u32[]{:S(2)}, u32[]{:S(2)}) collective-permute-start(bf16[128,896]{0,1:T(8,128)(2,1)} %constant_dynamic-slice_fusion), channel_id=1, source_target_pairs={{0,0},{1,1},{2,4},{3,5},{4,256},{5,257},{6,260},{7,261},{8,8},{9,9... | collective-permute-start | bytes 688136 | tf_op jit(solution)/shard_map/ppermute | solution.py:31
  65.1 0.2 convert_reduce_fusion
  65.3 1.4 convolution_convert_fusion.1
  66.7 23.3 %all-to-all-start.2 = ((bf16[32,16,896]{2,1,0:T(8,128)(2,1)}), bf16[32,16,896]{2,1,0:T(8,128)(2,1)}, u32[]{:S(2)}, u32[]{:S(2)}) async-start(bf16[32,16,896]{2,1,0:T(8,128)(2,1)} %bitcast.54), calls=%async_computation.2 | async-start | bytes 1835008 | tf_op jit(solution)/shard_map/all_to_all | solution.py:124
  90.0 0.2 convert_reduce_fusion.1
  90.2 0.4 convolution_convert_fusion.2
  90.6 9.8 %collective-permute-start.1 = (bf16[128,896]{1,0:T(8,128)(2,1)S(1)}, bf16[128,896]{1,0:T(8,128)(2,1)S(1)}, u32[]{:S(2)}, u32[]{:S(2)}) collective-permute-start(bf16[128,896]{1,0:T(8,128)(2,1)S(1)} %convolution_convert_fusion.2), channel_id=1, source_target_pairs={{0,256},{1,257},{2,258},{3,259},{4,260},{5,261},{6,262},{7,263},{8... | collective-permute-start | bytes 688136 | tf_op jit(solution)/shard_map/ppermute | solution.py:31
  100.4 0.7 collective-permute-start
  101.1 0.1 eq.165
  101.2 21.0 %collective-permute-done.1 = bf16[128,896]{1,0:T(8,128)(2,1)S(1)} collective-permute-done((bf16[128,896]{1,0:T(8,128)(2,1)S(1)}, bf16[128,896]{1,0:T(8,128)(2,1)S(1)}, u32[]{:S(2)}, u32[]{:S(2)}) %collective-permute-start.1) | collective-permute-done | bytes 229408 | tf_op jit(solution)/shard_map/ppermute | solution.py:31
  122.2 0.1 add.524
  122.3 1.9 %collective-permute-start.2 = (bf16[128,896]{1,0:T(8,128)(2,1)S(1)}, bf16[128,896]{1,0:T(8,128)(2,1)S(1)}, u32[]{:S(2)}, u32[]{:S(2)}) collective-permute-start(bf16[128,896]{1,0:T(8,128)(2,1)S(1)} %add.524), channel_id=1, source_target_pairs={{0,32},{32,0},{1,33},{33,1},{2,34},{34,2},{3,35},{35,3},{4,36},{36... | collective-permute-start | bytes 688136 | tf_op jit(solution)/shard_map/ppermute | solution.py:106
  124.2 3.9 %convolution_convert_fusion = bf16[1188,896]{1,0:T(8,128)(2,1)} fusion(bf16[512,896]{1,0:T(8,128)(2,1)} %bitcast.19, s32[512]{0:T(512)S(1)} %eq.165), kind=kOutput, calls=%fused_computation.2 | convolution fusion | flops 1091667456 | bytes 3048448 | tf_op jit(solution)/shard_map/dot_general | solution.py:127
  128.2 14.8 %all-gather = bf16[512,896]{1,0:T(8,128)(2,1)S(1)} all-gather(bf16[128,896]{1,0:T(8,128)(2,1)S(1)} %add.525), channel_id=2, replica_groups=mesh['z_hi'=2,'y'=4,'core'=2,'x'=4,'z_lo'=8] {'y'}, dimensions={0}, use_global_device_ids=true | all-gather | bytes 1146880 | tf_op jit(solution)/shard_map/all_gather | solution.py:107
  143.1 0.1 dynamic-slice_bitcast_fusion.3
  143.1 1.0 pad_maximum_fusion
  (19 shorter events, 0.2 us)
Async XLA Ops:
  0.6 30.6 %copy-start = (bf16[1188,896]{1,0:T(8,128)(2,1)S(1)}, bf16[1188,896]{1,0:T(8,128)(2,1)}, u32[]{:S(2)}) copy-start(bf16[1188,896]{1,0:T(8,128)(2,1)} %param.4) | copy-start | bytes 6386692
  2.1 26.9 %all-to-all-start = ((s32[32,1,128]{2,1,0:T(1,128)}), s32[32,1,128]{2,1,0:T(1,128)S(1)}, u32[]{:S(2)}, u32[]{:S(2)}) async-start(s32[32,1,128]{2,1,0:T(1,128)} %broadcast_in_dim.37), calls=%async_computation | async-start | bytes 32768 | tf_op jit(solution)/shard_map/all_to_all | solution.py:75
  34.4 32.3 %all-to-all-start.1 = ((bf16[32,16,896]{2,1,0:T(8,128)(2,1)}), bf16[32,16,896]{2,1,0:T(8,128)(2,1)S(1)}, u32[]{:S(2)}, u32[]{:S(2)}) async-start(bf16[32,16,896]{2,1,0:T(8,128)(2,1)} %broadcast_select_fusion), calls=%async_computation.1 | async-start | bytes 1835008 | tf_op jit(solution)/shard_map/all_to_all | solution.py:92
  63.5 1.8 %collective-permute-start.3 = (bf16[128,896]{0,1:T(8,128)(2,1)}, bf16[128,896]{0,1:T(8,128)(2,1)S(1)}, u32[]{:S(2)}, u32[]{:S(2)}) collective-permute-start(bf16[128,896]{0,1:T(8,128)(2,1)} %constant_dynamic-slice_fusion), channel_id=1, source_target_pairs={{0,0},{1,1},{2,4},{3,5},{4,256},{5,257},{6,260},{7,261},{8,8},{9,9... | collective-permute-start | bytes 688136 | tf_op jit(solution)/shard_map/ppermute | solution.py:31
  66.7 57.5 %all-to-all-start.2 = ((bf16[32,16,896]{2,1,0:T(8,128)(2,1)}), bf16[32,16,896]{2,1,0:T(8,128)(2,1)}, u32[]{:S(2)}, u32[]{:S(2)}) async-start(bf16[32,16,896]{2,1,0:T(8,128)(2,1)} %bitcast.54), calls=%async_computation.2 | async-start | bytes 1835008 | tf_op jit(solution)/shard_map/all_to_all | solution.py:124
  90.6 31.7 %collective-permute-start.1 = (bf16[128,896]{1,0:T(8,128)(2,1)S(1)}, bf16[128,896]{1,0:T(8,128)(2,1)S(1)}, u32[]{:S(2)}, u32[]{:S(2)}) collective-permute-start(bf16[128,896]{1,0:T(8,128)(2,1)S(1)} %convolution_convert_fusion.2), channel_id=1, source_target_pairs={{0,256},{1,257},{2,258},{3,259},{4,260},{5,261},{6,262},{7,263},{8... | collective-permute-start | bytes 688136 | tf_op jit(solution)/shard_map/ppermute | solution.py:31
  100.4 21.8 %collective-permute-start = (bf16[128,896]{1,0:T(8,128)(2,1)S(1)}, bf16[128,896]{1,0:T(8,128)(2,1)S(1)}, u32[]{:S(2)}, u32[]{:S(2)}) collective-permute-start(bf16[128,896]{1,0:T(8,128)(2,1)S(1)} %convolution_convert_fusion.2), channel_id=1, source_target_pairs={{0,0},{1,1},{2,2},{3,3},{4,4},{5,5},{6,6},{7,7},{8,8},{9,9},{10,10... | collective-permute-start | bytes 688136 | tf_op jit(solution)/shard_map/ppermute | solution.py:31
  122.3 5.9 %collective-permute-start.2 = (bf16[128,896]{1,0:T(8,128)(2,1)S(1)}, bf16[128,896]{1,0:T(8,128)(2,1)S(1)}, u32[]{:S(2)}, u32[]{:S(2)}) collective-permute-start(bf16[128,896]{1,0:T(8,128)(2,1)S(1)} %add.524), channel_id=1, source_target_pairs={{0,32},{32,0},{1,33},{33,1},{2,34},{34,2},{3,35},{35,3},{4,36},{36... | collective-permute-start | bytes 688136 | tf_op jit(solution)/shard_map/ppermute | solution.py:106
where the time goes:
time: 145 us; the launch traced here: 144 us
  starting transfers between devices  59.7 us (41%)
  blocking collectives  36.4 us (25%)
  waiting for transfers between devices  32.1 us (22%)
  matrix products  5.85 us (4%)
  local copies, waits for them, and re-layouts  5.02 us (3%)
  other arithmetic  4.18 us (3%)
    all_to_all x1, starting transfers between devices, body(): lax.all_to_all(packed.reshape(32, SLOTS, width), PLANE, 0, 0, tiled=True)  23.3 us
    all_gather x1, blocking collectives, body(): halves = lax.all_gather(out_grad, ('y', 'core'), axis=1, tiled=True)  21.6 us
    ppermute x3, waiting for transfers between devices, move(): return lax.ppermute(values, NAMES, pairs)  21.1 us
    all_to_all x1, starting transfers between devices, body(): lax.all_to_all(jnp.broadcast_to(token_ids[None], (32, tokens)), GROUPS, 0...  15.7 us
    all_gather x1, blocking collectives, body(): whole = lax.all_gather(quarter, 'y')  14.8 us
    ppermute x3, starting transfers between devices, move(): return lax.ppermute(values, NAMES, pairs)  12.1 us
    all_to_all x1, waiting for transfers between devices, body(): lax.all_to_all(jnp.broadcast_to(token_ids[None], (32, tokens)), GROUPS, 0...  11 us
    all_to_all x1, starting transfers between devices, body(): lax.all_to_all(fetched.reshape(32, SLOTS, width), PLANE, 0, 0, tiled=True)  6.71 us
  transfers between devices with their start and end apart: 7, of which 2 were waited for; matrix products, arithmetic and copies ran while one was open for 5% of the time, Pallas kernels for 0%

commit v1 on v0

--- a/solution.py
+++ b/solution.py
@@ -112,7 +112,10 @@
         ],
         axis=1,
     )
-    halves = lax.all_gather(out_grad, ("y", "core"), axis=1, tiled=True)
+    halves = jnp.concatenate(
+        lax.all_to_all(jnp.stack([out_grad] * lax.axis_size(("y", "core"))), ("y", "core"), 0, 0),
+        axis=1,
+    )
     which = (place ^ z_lo) % 2
     piece = lax.dynamic_slice(halves, (0, which * width), (tokens, width))
     piece = move(piece, grad_target)

time: 145 us -> 133 us (0.917)
  the two profiles are of different devices: /device:TPU:2 before, /device:TPU:4 now
where the time goes in v1:
time: 133 us; the launch traced here: 132 us
  starting transfers between devices  50.5 us (38%)
  waiting for transfers between devices  38.8 us (29%)
  blocking collectives  22.8 us (17%)
  local copies, waits for them, and re-layouts  7.28 us (5%)
  other arithmetic  7.1 us (5%)
  matrix products  4.67 us (4%)
    all_gather x1, blocking collectives, body(): whole = lax.all_gather(quarter, 'y')  22.8 us
    all_to_all x1, starting transfers between devices, body(): lax.all_to_all(jnp.broadcast_to(token_ids[None], (32, tokens)), GROUPS, 0...  15.7 us
    ppermute x3, waiting for transfers between devices, move(): return lax.ppermute(values, NAMES, pairs)  15.1 us
    all_to_all x1, waiting for transfers between devices, body(): lax.all_to_all(fetched.reshape(32, SLOTS, width), PLANE, 0, 0, tiled=True)  10.7 us
    ppermute x3, starting transfers between devices, move(): return lax.ppermute(values, NAMES, pairs)  10.5 us
    all_to_all x1, waiting for transfers between devices, body(): lax.all_to_all(jnp.broadcast_to(token_ids[None], (32, tokens)), GROUPS, 0...  10.1 us
    all_to_all x1, starting transfers between devices, body(): lax.all_to_all(packed.reshape(32, SLOTS, width), PLANE, 0, 0, tiled=True)  8.17 us
    all_to_all x1, starting transfers between devices, body(): lax.all_to_all(fetched.reshape(32, SLOTS, width), PLANE, 0, 0, tiled=True)  5.87 us
  transfers between devices with their start and end apart: 8, of which 4 were waited for; matrix products, arithmetic and copies ran while one was open for 10% of the time, Pallas kernels for 0%

profile of v1, /device:TPU:4, one launch (start us, length us, event | category | flops | bytes accessed | tf_op | source)
XLA Modules:
  0.0 132.1 jit_solution(4822787026784274148)
XLA Ops:
  0.6 1.4 %broadcast_in_dim.37 = s32[32,1,128]{2,1,0:T(1,128)} broadcast(s32[128]{0:T(128)} %param.3), dimensions={2} | broadcast | bytes 16896 | tf_op jit(solution)/shard_map/broadcast_in_dim | solution.py:76
  2.1 15.7 %all-to-all-start = ((s32[32,1,128]{2,1,0:T(1,128)}), s32[32,1,128]{2,1,0:T(1,128)S(1)}, u32[]{:S(2)}, u32[]{:S(2)}) async-start(s32[32,1,128]{2,1,0:T(1,128)} %broadcast_in_dim.37), calls=%async_computation | async-start | bytes 32768 | tf_op jit(solution)/shard_map/all_to_all | solution.py:75
  18.0 10.1 %all-to-all-done = s32[32,1,128]{2,1,0:T(1,128)S(1)} async-done(((s32[32,1,128]{2,1,0:T(1,128)}), s32[32,1,128]{2,1,0:T(1,128)S(1)}, u32[]{:S(2)}, u32[]{:S(2)}) %all-to-all-start) | async-done | bytes 16416 | tf_op jit(solution)/shard_map/all_to_all | solution.py:75
  28.1 1.6 %stack.2 = bf16[8,128,224]{1,2,0:T(8,128)(2,1)} broadcast(bf16[128,224]{0,1:T(8,128)(2,1)} %param.5), dimensions={1,2} | broadcast | bytes 516096 | tf_op jit(solution)/shard_map/stack | solution.py:116
  29.7 4.5 %all-to-all-start.2 = ((bf16[8,128,224]{1,2,0:T(8,128)(2,1)}), bf16[8,128,224]{1,2,0:T(8,128)(2,1)S(1)}, u32[]{:S(2)}, u32[]{:S(2)}) async-start(bf16[8,128,224]{1,2,0:T(8,128)(2,1)} %stack.2), calls=%async_computation.2 | async-start | bytes 917504 | tf_op jit(solution)/shard_map/all_to_all | solution.py:116
  34.2 0.6 gather_fusion
  34.9 0.1 fusion.11
  35.0 0.1 convolution_convert_fusion.3
  35.2 1.2 select_reduce_fusion
  36.3 0.6 copy-done.1
  37.1 2.1 %gather_fusion.1 = bf16[512,896]{1,0:T(8,128)(2,1)S(1)} fusion(bf16[1188,896]{1,0:T(8,128)(2,1)S(1)} %copy-done, s32[1024]{0:T(1024)S(1)} %pad_clamp_fusion), kind=kCustom, calls=%fused_computation.1 | custom fusion | bytes 1837056 | tf_op jit(solution)/shard_map/jit(_take)/gather | solution.py:91
  39.1 0.7 broadcast_compare_fusion
  39.9 1.1 broadcast_select_fusion
  41.0 2.9 %all-to-all-done.2 = bf16[8,128,224]{1,2,0:T(8,128)(2,1)S(1)} async-done(((bf16[8,128,224]{1,2,0:T(8,128)(2,1)}), bf16[8,128,224]{1,2,0:T(8,128)(2,1)S(1)}, u32[]{:S(2)}, u32[]{:S(2)}) %all-to-all-start.2) | async-done | bytes 458784 | tf_op jit(solution)/shard_map/all_to_all | solution.py:116
  43.8 5.9 %all-to-all-start.1 = ((bf16[32,16,896]{2,1,0:T(8,128)(2,1)}), bf16[32,16,896]{2,1,0:T(8,128)(2,1)S(1)}, u32[]{:S(2)}, u32[]{:S(2)}) async-start(bf16[32,16,896]{2,1,0:T(8,128)(2,1)} %broadcast_select_fusion), calls=%async_computation.1 | async-start | bytes 1835008 | tf_op jit(solution)/shard_map/all_to_all | solution.py:92
  49.8 0.6 multiply_add_fusion
  50.4 0.2 convert_reduce_fusion.1
  50.6 0.7 constant_dynamic-slice_fusion
  51.3 1.6 %collective-permute-start.3 = (bf16[128,896]{0,1:T(8,128)(2,1)}, bf16[128,896]{0,1:T(8,128)(2,1)S(1)}, u32[]{:S(2)}, u32[]{:S(2)}) collective-permute-start(bf16[128,896]{0,1:T(8,128)(2,1)} %constant_dynamic-slice_fusion), channel_id=1, source_target_pairs={{0,0},{1,1},{2,4},{3,5},{4,256},{5,257},{6,260},{7,261},{8,8},{9,9... | collective-permute-start | bytes 688136 | tf_op jit(solution)/shard_map/ppermute | solution.py:31
  52.9 10.7 %all-to-all-done.1 = bf16[32,16,896]{2,1,0:T(8,128)(2,1)S(1)} async-done(((bf16[32,16,896]{2,1,0:T(8,128)(2,1)}), bf16[32,16,896]{2,1,0:T(8,128)(2,1)S(1)}, u32[]{:S(2)}, u32[]{:S(2)}) %all-to-all-start.1) | async-done | bytes 917536 | tf_op jit(solution)/shard_map/all_to_all | solution.py:92
  63.5 0.3 convolution_convert_fusion.2
  63.9 8.2 %collective-permute-start.1 = (bf16[128,896]{1,0:T(8,128)(2,1)S(1)}, bf16[128,896]{1,0:T(8,128)(2,1)S(1)}, u32[]{:S(2)}, u32[]{:S(2)}) collective-permute-start(bf16[128,896]{1,0:T(8,128)(2,1)S(1)} %convolution_convert_fusion.2), channel_id=1, source_target_pairs={{0,256},{1,257},{2,258},{3,259},{4,260},{5,261},{6,262},{7,263},{8... | collective-permute-start | bytes 688136 | tf_op jit(solution)/shard_map/ppermute | solution.py:31
  72.1 0.7 collective-permute-start
  72.8 0.9 convert_reduce_fusion
  73.8 15.1 %collective-permute-done.1 = bf16[128,896]{1,0:T(8,128)(2,1)S(1)} collective-permute-done((bf16[128,896]{1,0:T(8,128)(2,1)S(1)}, bf16[128,896]{1,0:T(8,128)(2,1)S(1)}, u32[]{:S(2)}, u32[]{:S(2)}) %collective-permute-start.1) | collective-permute-done | bytes 229408 | tf_op jit(solution)/shard_map/ppermute | solution.py:31
  89.0 5.9 %collective-permute-start.2 = (bf16[128,896]{1,0:T(8,128)(2,1)S(1)}, bf16[128,896]{1,0:T(8,128)(2,1)}, u32[]{:S(2)}, u32[]{:S(2)}) collective-permute-start(bf16[128,896]{1,0:T(8,128)(2,1)S(1)} %add.524), channel_id=1, source_target_pairs={{0,32},{32,0},{1,33},{33,1},{2,34},{34,2},{3,35},{35,3},{4,36},{36... | collective-permute-start | bytes 688136 | tf_op jit(solution)/shard_map/ppermute | solution.py:106
  94.9 1.4 %convolution_convert_fusion.1 = bf16[512,896]{1,0:T(8,128)(2,1)} fusion(bf16[128,896]{0,1:T(8,128)(2,1)S(1)} %collective-permute-done.3, s32[128]{0:T(128)S(1)} %and_select_fusion.2), kind=kOutput, calls=%fused_computation.4 | convolution fusion | flops 118030336 | bytes 1147392 | tf_op jit(solution)/shard_map/dot_general | solution.py:124
  96.3 8.2 %all-to-all-start.3 = ((bf16[32,16,896]{2,1,0:T(8,128)(2,1)}), bf16[32,16,896]{2,1,0:T(8,128)(2,1)S(1)}, u32[]{:S(2)}, u32[]{:S(2)}) async-start(bf16[32,16,896]{2,1,0:T(8,128)(2,1)} %bitcast.20), calls=%async_computation.3 | async-start | bytes 1835008 | tf_op jit(solution)/shard_map/all_to_all | solution.py:127
  104.5 1.0 add.525
  105.5 22.8 %all-gather = bf16[512,896]{1,0:T(8,128)(2,1)S(1)} all-gather(bf16[128,896]{1,0:T(8,128)(2,1)S(1)} %add.525), channel_id=2, replica_groups=mesh['z_hi'=2,'y'=4,'core'=2,'x'=4,'z_lo'=8] {'y'}, dimensions={0}, use_global_device_ids=true | all-gather | bytes 1146880 | tf_op jit(solution)/shard_map/all_gather | solution.py:107
  128.4 1.0 pad_maximum_fusion
  129.4 2.8 %convolution_convert_fusion = bf16[1188,896]{1,0:T(8,128)(2,1)} fusion(bf16[512,896]{1,0:T(8,128)(2,1)S(1)} %bitcast.59, s32[512]{0:T(512)S(1)} %eq.165), kind=kOutput, calls=%fused_computation.2 | convolution fusion | flops 1091667456 | bytes 3048448 | tf_op jit(solution)/shard_map/dot_general | solution.py:130
  (23 shorter events, 0.7 us)
Async XLA Ops:
  0.6 36.4 %copy-start = (bf16[1188,896]{1,0:T(8,128)(2,1)S(1)}, bf16[1188,896]{1,0:T(8,128)(2,1)}, u32[]{:S(2)}) copy-start(bf16[1188,896]{1,0:T(8,128)(2,1)} %param.4) | copy-start | bytes 6386692
  2.1 26.0 %all-to-all-start = ((s32[32,1,128]{2,1,0:T(1,128)}), s32[32,1,128]{2,1,0:T(1,128)S(1)}, u32[]{:S(2)}, u32[]{:S(2)}) async-start(s32[32,1,128]{2,1,0:T(1,128)} %broadcast_in_dim.37), calls=%async_computation | async-start | bytes 32768 | tf_op jit(solution)/shard_map/all_to_all | solution.py:75
  29.7 14.1 %all-to-all-start.2 = ((bf16[8,128,224]{1,2,0:T(8,128)(2,1)}), bf16[8,128,224]{1,2,0:T(8,128)(2,1)S(1)}, u32[]{:S(2)}, u32[]{:S(2)}) async-start(bf16[8,128,224]{1,2,0:T(8,128)(2,1)} %stack.2), calls=%async_computation.2 | async-start | bytes 917504 | tf_op jit(solution)/shard_map/all_to_all | solution.py:116
  36.3 0.6 copy-start.1
  43.8 19.7 %all-to-all-start.1 = ((bf16[32,16,896]{2,1,0:T(8,128)(2,1)}), bf16[32,16,896]{2,1,0:T(8,128)(2,1)S(1)}, u32[]{:S(2)}, u32[]{:S(2)}) async-start(bf16[32,16,896]{2,1,0:T(8,128)(2,1)} %broadcast_select_fusion), calls=%async_computation.1 | async-start | bytes 1835008 | tf_op jit(solution)/shard_map/all_to_all | solution.py:92
  51.3 43.6 %collective-permute-start.3 = (bf16[128,896]{0,1:T(8,128)(2,1)}, bf16[128,896]{0,1:T(8,128)(2,1)S(1)}, u32[]{:S(2)}, u32[]{:S(2)}) collective-permute-start(bf16[128,896]{0,1:T(8,128)(2,1)} %constant_dynamic-slice_fusion), channel_id=1, source_target_pairs={{0,0},{1,1},{2,4},{3,5},{4,256},{5,257},{6,260},{7,261},{8,8},{9,9... | collective-permute-start | bytes 688136 | tf_op jit(solution)/shard_map/ppermute | solution.py:31
  63.9 25.0 %collective-permute-start.1 = (bf16[128,896]{1,0:T(8,128)(2,1)S(1)}, bf16[128,896]{1,0:T(8,128)(2,1)S(1)}, u32[]{:S(2)}, u32[]{:S(2)}) collective-permute-start(bf16[128,896]{1,0:T(8,128)(2,1)S(1)} %convolution_convert_fusion.2), channel_id=1, source_target_pairs={{0,256},{1,257},{2,258},{3,259},{4,260},{5,261},{6,262},{7,263},{8... | collective-permute-start | bytes 688136 | tf_op jit(solution)/shard_map/ppermute | solution.py:31
  72.1 16.8 %collective-permute-start = (bf16[128,896]{1,0:T(8,128)(2,1)S(1)}, bf16[128,896]{1,0:T(8,128)(2,1)S(1)}, u32[]{:S(2)}, u32[]{:S(2)}) collective-permute-start(bf16[128,896]{1,0:T(8,128)(2,1)S(1)} %convolution_convert_fusion.2), channel_id=1, source_target_pairs={{0,0},{1,1},{2,2},{3,3},{4,4},{5,5},{6,6},{7,7},{8,8},{9,9},{10,10... | collective-permute-start | bytes 688136 | tf_op jit(solution)/shard_map/ppermute | solution.py:31
  89.0 15.5 %collective-permute-start.2 = (bf16[128,896]{1,0:T(8,128)(2,1)S(1)}, bf16[128,896]{1,0:T(8,128)(2,1)}, u32[]{:S(2)}, u32[]{:S(2)}) collective-permute-start(bf16[128,896]{1,0:T(8,128)(2,1)S(1)} %add.524), channel_id=1, source_target_pairs={{0,32},{32,0},{1,33},{33,1},{2,34},{34,2},{3,35},{35,3},{4,36},{36... | collective-permute-start | bytes 688136 | tf_op jit(solution)/shard_map/ppermute | solution.py:106
  96.3 33.1 %all-to-all-start.3 = ((bf16[32,16,896]{2,1,0:T(8,128)(2,1)}), bf16[32,16,896]{2,1,0:T(8,128)(2,1)S(1)}, u32[]{:S(2)}, u32[]{:S(2)}) async-start(bf16[32,16,896]{2,1,0:T(8,128)(2,1)} %bitcast.20), calls=%async_computation.3 | async-start | bytes 1835008 | tf_op jit(solution)/shard_map/all_to_all | solution.py:127
